TPU v7x, 32 devices: a whole 2x2x4 slice. The times are simulated.
32 devices in a mesh: ga: 8 (over z, core), gp: 4 (over y, x).
Axes of the slice: x: 2, y: 2, z: 4, core: 2. Of those that a mesh axis runs over, the one named last changes fastest.
Arguments:
- matel: bfloat16 [16, 16, 100352], P('ga', None, 'gp'), may hold values from -0.01953125 to 0.01953125
- pole_amp: bfloat16 [1024, 100352], P('ga', 'gp'), may hold values from -6 to 6
- pole_freq: bfloat16 [1024, 100352], P('ga', 'gp'), may hold values from 0.5 to 4
- band_energy: float32 [16], replicated, may hold values from -3 to 3
- energies: float32 [3], replicated, may hold values from -2 to 2
- owner: int32 [5], replicated, may hold values from 0 to 7
- slot: int32 [5], replicated, may hold values from 0 to 1
Outputs:
- sigma: float32 [3, 16, 16], replicated
Inputs may be any that keep to these rules, and one draw needn't show every extreme that they name: `slot`: position among the 2 bands stored by that row.
All inputs are finite; a program needn't handle non-finite values.
Results may differ from a plain program's by a relative error of at most 0.0029.
Values may be sent and summed in bfloat16 or wider, within the bound.
No kernel may reach another device: no remote copies, remote signals or barrier semaphores. Data moves between devices by JAX's collectives and lax.ppermute only.
A program may use at most 128 MiB of HBM per device.

v0:
```python
import jax
import jax.numpy as jnp
from jax import lax
from jax.sharding import PartitionSpec as P


def from_root(shard, axis, root):
    mine = lax.axis_index(axis) == root
    return lax.psum(jnp.where(mine, shard, jnp.zeros_like(shard)), axis)


def shards(matel, pole_amp, pole_freq, band_energy, energies, owner, slot):
    held_bands = matel.shape[0]
    states = matel.shape[1]
    cols_tile = matel.shape[2]
    rows_tile = pole_amp.shape[0]
    row_index = lax.axis_index("ga")
    first_row = row_index * rows_tile
    source = first_row // cols_tile
    offset = first_row % cols_tile
    amplitude = pole_amp.astype(jnp.float32)
    frequency = pole_freq.astype(jnp.float32)
    numerator = amplitude * frequency
    squared = frequency * frequency
    labels = jnp.arange(band_energy.shape[0], dtype=jnp.int32)
    partial_value = jnp.zeros((energies.shape[0], states, states), jnp.float32)
    for band_slot in range(owner.shape[0]):
        own_piece = lax.dynamic_index_in_dim(matel, slot[band_slot], 0, keepdims=False)
        column = from_root(own_piece, "ga", owner[band_slot])
        window_rows = lax.dynamic_slice_in_dim(column, offset, rows_tile, 1)
        row_piece = from_root(window_rows, "gp", source)
        band_level = jnp.sum(
            jnp.where(labels == owner[band_slot] * held_bands + slot[band_slot], band_energy, 0.0)
        )
        detuning = energies[:, None, None] - band_level
        pole_value = (numerator / (detuning * detuning + squared)).astype(jnp.bfloat16)
        folded = jnp.einsum("egk,sk->esg", pole_value, column, preferred_element_type=jnp.float32)
        partial_value = partial_value + jnp.einsum(
            "tg,esg->ets", row_piece.astype(jnp.float32), folded, precision=lax.Precision.HIGHEST
        )
    sigma_sum = lax.psum(partial_value, ("ga", "gp"))
    return sigma_sum


def solution(mesh):
    return jax.shard_map(
        shards,
        mesh=mesh,
        in_specs=(P("ga", None, "gp"), P("ga", "gp"), P("ga", "gp"), P(), P(), P(), P()),
        out_specs=P(),
        check_vma=False,
    )
```

profile of v0, /device:TPU:0, one launch (start us, length us, event | category | flops | bytes accessed | tf_op | source)
XLA Modules:
  0.0 232.1 jit_solution(8351332103755635350)
XLA Ops:
  6.5 0.0 all-reduce.4.cloned.1.call-start
  6.5 1.5 fusion.27
  14.1 1.5 fusion.28
  21.9 4.5 %select_bitcast_fusion = (bf16[16,25088]{1,0:T(8,128)(2,1)}, bf16[16,25088]{1,0:T(8,128)(2,1)}, bf16[16,25088]{1,0:T(8,128)(2,1)}, bf16[16,25088]{1,0:T(8,128)(2,1)}, bf16[16,25088]{1,0:T(8,128)(2,1)}) fusion(bf16[2,16,25088]{2,1,0:T(8,128)(2,1)} %param.7, s32[]{:T(128)S(6)} %select_n.150, pred[]{:T(512)S(6)} %eq.67, s32[]{:T(128)S(6)} %select_n.138, ...), kind=kLoop, calls=%fused_computation.27 | loop fusion | flops 2007040 | bytes 8028185 | tf_op jit(solution)/shard_map/jit(_where)/select_n | solution.py:9
  26.3 0.0 all-reduce.4.cloned.1.call-update
  26.4 0.0 copy-start.6
  26.4 0.0 copy-start.7
  26.4 12.5 %convert_multiply_fusion.1 = (f32[128,25088]{1,0:T(8,128)}, f32[128,25088]{1,0:T(8,128)}) fusion(bf16[128,25088]{1,0:T(8,128)(2,1)} %param.9, bf16[128,25088]{1,0:T(8,128)(2,1)} %param.8), kind=kLoop, calls=%fused_computation.11 | loop fusion | flops 12845056 | bytes 38535168 | tf_op jit(solution)/shard_map/mul | solution.py:23
  45.2 0.0 copy-done.6
  45.3 0.6 fusion.26
  45.9 0.0 copy-done.7
  45.9 3.6 %subtract_multiply_fusion = (f32[3]{0:T(128)S(1)}, f32[3]{0:T(128)S(1)}, f32[3]{0:T(128)S(1)}, f32[3]{0:T(128)}, f32[3]{0:T(128)S(1)}) fusion(f32[3]{0:T(128)S(1)} %copy-done.7, f32[]{:T(128)} %get-tuple-element.5, f32[]{:T(128)} %get-tuple-element.6, f32[]{:T(128)} %get-tuple-element.7, f32[]{:T(128)} %get-tuple-element.8, f32[]{:T(128)} %get-tuple-element.9), kind=kLoop, calls=%fused_computation.53 | loop fusion | flops 30 | bytes 92 | tf_op jit(solution)/shard_map/mul | solution.py:36
  49.5 73.6 %all-reduce.4.cloned.1.call-done = (bf16[16,25088]{1,0:T(8,128)(2,1)}, bf16[16,25088]{1,0:T(8,128)(2,1)}, bf16[16,25088]{1,0:T(8,128)(2,1)}, bf16[16,25088]{1,0:T(8,128)(2,1)}, bf16[16,25088]{1,0:T(8,128)(2,1)}) async-done(((bf16[16,25088]{1,0:T(8,128)(2,1)}, bf16[16,25088]{1,0:T(8,128)(2,1)}, bf16[16,25088]{1,0:T(8,128)(2,1)}, bf16[16,25088]{1,0:T(8,128)(2,1)}, bf16[16,25088]{1,0:T(8,128)(2,1)}), ...) | async-done | bytes 4014096 | tf_op jit(solution)/shard_map/psum | solution.py:9
  123.1 1.4 dynamic-slice_select_fusion.4
  124.5 1.4 dynamic-slice_select_fusion.2
  125.8 0.0 copy-start
  125.8 0.0 copy-start.1
  125.8 12.4 %fusion.8 = f32[3,16,128]{2,1,0:T(8,128)} fusion(f32[3]{0:T(128)S(1)} %get-tuple-element.29, f32[128,25088]{1,0:T(8,128)} %get-tuple-element.21, f32[128,25088]{1,0:T(8,128)} %get-tuple-element.20, bf16[16,25088]{1,0:T(8,128)(2,1)} %get-tuple-element.11), kind=kOutput, calls=%fused_computation.15 | convolution fusion | flops 337182720 | bytes 26517516 | tf_op jit(solution)/shard_map/egk,sk->esg/dot_general | solution.py:37
  138.3 0.0 copy-done
  138.3 3.5 %copy-done.1 = f32[128,25088]{1,0:T(8,128)S(1)} copy-done((f32[128,25088]{1,0:T(8,128)S(1)}, f32[128,25088]{1,0:T(8,128)}, u32[]{:S(2)}) %copy-start.1) | copy-done | bytes 12845080
  141.8 0.0 copy-start.9
  141.8 6.9 %fusion.7 = f32[3,16,128]{2,1,0:T(8,128)S(1)} fusion(f32[3]{0:T(128)S(1)} %get-tuple-element.28, f32[128,25088]{1,0:T(8,128)S(1)} %copy-done.1, f32[128,25088]{1,0:T(8,128)S(1)} %copy-done, bf16[16,25088]{1,0:T(8,128)(2,1)} %get-tuple-element.12), kind=kOutput, calls=%fused_computation.14 | convolution fusion | flops 337182720 | bytes 26517516 | tf_op jit(solution)/shard_map/egk,sk->esg/dot_general | solution.py:37
  148.7 0.0 copy-done.9
  148.7 0.8 dynamic-slice_select_fusion
  149.5 6.8 %fusion.6 = f32[3,16,128]{2,1,0:T(8,128)S(1)} fusion(f32[3]{0:T(128)S(1)} %get-tuple-element.31, f32[128,25088]{1,0:T(8,128)S(1)} %copy-done.1, f32[128,25088]{1,0:T(8,128)S(1)} %copy-done, bf16[16,25088]{1,0:T(8,128)(2,1)} %get-tuple-element.13), kind=kOutput, calls=%fused_computation.13 | convolution fusion | flops 337182720 | bytes 26517516 | tf_op jit(solution)/shard_map/egk,sk->esg/dot_general | solution.py:37
  156.3 0.0 copy-start.8
  156.3 5.2 %fusion.5 = f32[3,16,128]{2,1,0:T(8,128)S(1)} fusion(f32[3]{0:T(128)S(1)} %get-tuple-element.27, f32[128,25088]{1,0:T(8,128)S(1)} %copy-done.1, f32[128,25088]{1,0:T(8,128)S(1)} %copy-done, bf16[16,25088]{1,0:T(8,128)(2,1)S(1)} %copy-done.9), kind=kOutput, calls=%fused_computation.12 | convolution fusion | flops 337182720 | bytes 26517516 | tf_op jit(solution)/shard_map/egk,sk->esg/dot_general | solution.py:37
  161.5 0.0 copy-done.8
  161.5 0.0 copy-start.3
  161.5 0.0 copy-start.4
  161.5 0.0 copy-start.5
  161.5 0.0 copy-start.2
  161.5 6.8 %fusion.9 = f32[3,16,128]{2,1,0:T(8,128)S(1)} fusion(f32[128,25088]{1,0:T(8,128)S(1)} %copy-done.1, f32[3]{0:T(128)S(1)} %copy-done.8, f32[128,25088]{1,0:T(8,128)S(1)} %copy-done, bf16[16,25088]{1,0:T(8,128)(2,1)} %get-tuple-element.10), kind=kOutput, calls=%fused_computation.16 | convolution fusion | flops 337182720 | bytes 26517516 | tf_op jit(solution)/shard_map/egk,sk->esg/dot_general | solution.py:37
  168.4 0.0 copy-done.3
  168.4 0.0 copy-done.4
  168.4 0.0 copy-done.5
  168.4 16.2 %all-reduce.1 = (bf16[16,128]{1,0:T(8,128)(2,1)S(1)}, bf16[16,128]{1,0:T(8,128)(2,1)S(1)}, bf16[16,128]{1,0:T(8,128)(2,1)S(1)}, bf16[16,128]{1,0:T(8,128)(2,1)S(1)}, bf16[16,128]{1,0:T(8,128)(2,1)S(1)}) all-reduce(bf16[16,128]{1,0:T(8,128)(2,1)S(1)} %copy-done.5, ...), channel_id=1, replica_groups=mesh['ga'=8,'gp'=4] {'gp'}, use_global_device_ids=true, to_apply=%region_2.3 | all-reduce | flops 10240 | bytes 40960 | tf_op jit(solution)/shard_map/psum | solution.py:9
  184.6 0.1 fusion.20
  184.7 0.0 copy-done.2
  184.7 0.1 convolution_add_fusion.3
  184.8 0.1 convolution_add_fusion.2
  185.0 0.1 convolution_add_fusion.1
  185.1 0.1 fusion.10
  185.3 39.3 %psum.87 = f32[3,16,16]{1,2,0:T(8,128)S(1)} all-reduce(f32[3,16,16]{1,2,0:T(8,128)S(1)} %fusion.10), channel_id=1, replica_groups=mesh['ga'=8,'gp'=4] {'ga','gp'}, use_global_device_ids=true, to_apply=%region_15.16 | all-reduce | flops 768 | bytes 6144 | tf_op jit(solution)/shard_map/psum | solution.py:41
  224.5 0.7 copy.8
Async XLA Ops:
  6.5 116.5 %all-reduce.4.cloned.1.call-start = ((), (), s32[]{:S(2)}) async-start(), calls=%async_computation | async-start | bytes 8028160 | tf_op jit(solution)/shard_map/psum | solution.py:9
  26.4 18.9 %copy-start.6 = (f32[16]{0:T(128)S(1)}, f32[16]{0:T(128)}, u32[]{:S(2)}) copy-start(f32[16]{0:T(128)} %param.10) | copy-start | bytes 196
  26.4 19.5 %copy-start.7 = (f32[3]{0:T(128)S(1)}, f32[3]{0:T(128)}, u32[]{:S(2)}) copy-start(f32[3]{0:T(128)} %param.11) | copy-start | bytes 40
  125.8 12.4 %copy-start = (f32[128,25088]{1,0:T(8,128)S(1)}, f32[128,25088]{1,0:T(8,128)}, u32[]{:S(2)}) copy-start(f32[128,25088]{1,0:T(8,128)} %get-tuple-element.20) | copy-start | bytes 38535172
  125.8 15.9 %copy-start.1 = (f32[128,25088]{1,0:T(8,128)S(1)}, f32[128,25088]{1,0:T(8,128)}, u32[]{:S(2)}) copy-start(f32[128,25088]{1,0:T(8,128)} %get-tuple-element.21) | copy-start | bytes 38535172
  141.8 6.9 %copy-start.9 = (bf16[16,25088]{1,0:T(8,128)(2,1)S(1)}, bf16[16,25088]{1,0:T(8,128)(2,1)}, u32[]{:S(2)}) copy-start(bf16[16,25088]{1,0:T(8,128)(2,1)} %get-tuple-element.14) | copy-start | bytes 2408452
  156.3 5.2 %copy-start.8 = (f32[3]{0:T(128)S(1)}, f32[3]{0:T(128)}, u32[]{:S(2)}) copy-start(f32[3]{0:T(128)} %get-tuple-element.30) | copy-start | bytes 40
  161.5 6.9 %copy-start.3 = (bf16[16,128]{1,0:T(8,128)(2,1)S(1)}, bf16[16,128]{1,0:T(8,128)(2,1)}, u32[]{:S(2)}) copy-start(bf16[16,128]{1,0:T(8,128)(2,1)} %get-tuple-element.44) | copy-start | bytes 12292
  161.5 6.9 %copy-start.4 = (bf16[16,128]{1,0:T(8,128)(2,1)S(1)}, bf16[16,128]{1,0:T(8,128)(2,1)}, u32[]{:S(2)}) copy-start(bf16[16,128]{1,0:T(8,128)(2,1)} %get-tuple-element.45) | copy-start | bytes 12292
  161.5 6.9 %copy-start.5 = (bf16[16,128]{1,0:T(8,128)(2,1)S(1)}, bf16[16,128]{1,0:T(8,128)(2,1)}, u32[]{:S(2)}) copy-start(bf16[16,128]{1,0:T(8,128)(2,1)} %dynamic-slice_select_fusion.4) | copy-start | bytes 12292
  161.5 23.2 %copy-start.2 = (f32[3,16,128]{2,1,0:T(8,128)S(1)}, f32[3,16,128]{2,1,0:T(8,128)}, u32[]{:S(2)}) copy-start(f32[3,16,128]{2,1,0:T(8,128)} %fusion.8) | copy-start | bytes 73732
Sparse Core Ops, SparseCore 0:
  26.5 96.5 all-reduce.3
where the time goes:
time: 233 us; the launch traced here: 232 us
  waiting for transfers between devices  73.6 us (32%)
  blocking collectives  55.4 us (24%)
  matrix products  38.8 us (17%)
  between operations  32.2 us (14%)
  other arithmetic  24.8 us (11%)
  local copies, waits for them, and re-layouts  7.2 us (3%)
    psum x1, waiting for transfers between devices, from_root(): return lax.psum(jnp.where(mine, shard, jnp.zeros_like(shard)), axis)  73.6 us
    psum x1, blocking collectives, shards(): sigma_sum = lax.psum(partial_value, ('ga', 'gp'))  39.3 us
    dot_general x5, matrix products, shards(): jnp.einsum('egk,sk->esg', pole_value, column, preferred_element_type=jnp....  38.2 us
    psum x1, blocking collectives, from_root(): return lax.psum(jnp.where(mine, shard, jnp.zeros_like(shard)), axis)  16.2 us
    mul x1, other arithmetic, shards(): numerator = amplitude * frequency  12.5 us
    select_n x4, other arithmetic, from_root(): return lax.psum(jnp.where(mine, shard, jnp.zeros_like(shard)), axis)  8 us
  transfers between devices with their start and end apart: 1, of which 1 were waited for; matrix products, arithmetic and copies ran while one was open for 7% of the time, Pallas kernels for 0%

commit v1 on v0

--- a/solution.py
+++ b/solution.py
@@ -38,7 +38,7 @@
         partial_value = partial_value + jnp.einsum(
             "tg,esg->ets", row_piece.astype(jnp.float32), folded, precision=lax.Precision.HIGHEST
         )
-    sigma_sum = lax.psum(partial_value, ("ga", "gp"))
+    sigma_sum = lax.psum(lax.psum(partial_value, "gp"), "ga")
     return sigma_sum
 
 

time: 233 us -> 234 us (level)
    psum x1 -> x2, blocking collectives: 39.3 us -> 40.2 us  [shards(): sigma_sum = lax.psum(lax.psum(partial_value, 'gp'), 'ga')]
where the time goes in v1:
time: 234 us; the launch traced here: 233 us
  waiting for transfers between devices  73.8 us (32%)
  blocking collectives  56.4 us (24%)
  matrix products  38.8 us (17%)
  between operations  31.9 us (14%)
  other arithmetic  24.8 us (11%)
  local copies, waits for them, and re-layouts  7.18 us (3%)
    psum x1, waiting for transfers between devices, from_root(): return lax.psum(jnp.where(mine, shard, jnp.zeros_like(shard)), axis)  73.7 us
    psum x2, blocking collectives, shards(): sigma_sum = lax.psum(lax.psum(partial_value, 'gp'), 'ga')  40.2 us
    dot_general x5, matrix products, shards(): jnp.einsum('egk,sk->esg', pole_value, column, preferred_element_type=jnp....  38.2 us
    psum x1, blocking collectives, from_root(): return lax.psum(jnp.where(mine, shard, jnp.zeros_like(shard)), axis)  16.2 us
    mul x1, other arithmetic, shards(): numerator = amplitude * frequency  12.5 us
    select_n x4, other arithmetic, from_root(): return lax.psum(jnp.where(mine, shard, jnp.zeros_like(shard)), axis)  8.02 us
  transfers between devices with their start and end apart: 1, of which 1 were waited for; matrix products, arithmetic and copies ran while one was open for 7% of the time, Pallas kernels for 0%

profile of v1, /device:TPU:0, one launch (start us, length us, event | category | flops | bytes accessed | tf_op | source)
XLA Modules:
  0.0 232.9 jit_solution(13836294585390810180)
XLA Ops:
  6.5 0.0 all-reduce.4.cloned.1.call-start
  6.5 1.4 fusion.27
  14.0 1.5 fusion.28
  21.7 4.5 %select_bitcast_fusion = (bf16[16,25088]{1,0:T(8,128)(2,1)}, bf16[16,25088]{1,0:T(8,128)(2,1)}, bf16[16,25088]{1,0:T(8,128)(2,1)}, bf16[16,25088]{1,0:T(8,128)(2,1)}, bf16[16,25088]{1,0:T(8,128)(2,1)}) fusion(bf16[2,16,25088]{2,1,0:T(8,128)(2,1)} %param.7, s32[]{:T(128)S(6)} %select_n.150, pred[]{:T(512)S(6)} %eq.67, s32[]{:T(128)S(6)} %select_n.138, ...), kind=kLoop, calls=%fused_computation.27 | loop fusion | flops 2007040 | bytes 8028185 | tf_op jit(solution)/shard_map/jit(_where)/select_n | solution.py:9
  26.2 0.0 all-reduce.4.cloned.1.call-update
  26.2 0.0 copy-start.6
  26.2 0.0 copy-start.7
  26.2 12.5 %convert_multiply_fusion.1 = (f32[128,25088]{1,0:T(8,128)}, f32[128,25088]{1,0:T(8,128)}) fusion(bf16[128,25088]{1,0:T(8,128)(2,1)} %param.9, bf16[128,25088]{1,0:T(8,128)(2,1)} %param.8), kind=kLoop, calls=%fused_computation.11 | loop fusion | flops 12845056 | bytes 38535168 | tf_op jit(solution)/shard_map/mul | solution.py:23
  44.9 0.0 copy-done.6
  45.0 0.6 fusion.26
  45.6 0.0 copy-done.7
  45.6 3.6 %subtract_multiply_fusion = (f32[3]{0:T(128)S(1)}, f32[3]{0:T(128)S(1)}, f32[3]{0:T(128)S(1)}, f32[3]{0:T(128)}, f32[3]{0:T(128)S(1)}) fusion(f32[3]{0:T(128)S(1)} %copy-done.7, f32[]{:T(128)} %get-tuple-element.5, f32[]{:T(128)} %get-tuple-element.6, f32[]{:T(128)} %get-tuple-element.7, f32[]{:T(128)} %get-tuple-element.8, f32[]{:T(128)} %get-tuple-element.9), kind=kLoop, calls=%fused_computation.53 | loop fusion | flops 30 | bytes 92 | tf_op jit(solution)/shard_map/mul | solution.py:36
  49.2 73.7 %all-reduce.4.cloned.1.call-done = (bf16[16,25088]{1,0:T(8,128)(2,1)}, bf16[16,25088]{1,0:T(8,128)(2,1)}, bf16[16,25088]{1,0:T(8,128)(2,1)}, bf16[16,25088]{1,0:T(8,128)(2,1)}, bf16[16,25088]{1,0:T(8,128)(2,1)}) async-done(((bf16[16,25088]{1,0:T(8,128)(2,1)}, bf16[16,25088]{1,0:T(8,128)(2,1)}, bf16[16,25088]{1,0:T(8,128)(2,1)}, bf16[16,25088]{1,0:T(8,128)(2,1)}, bf16[16,25088]{1,0:T(8,128)(2,1)}), ...) | async-done | bytes 4014096 | tf_op jit(solution)/shard_map/psum | solution.py:9
  122.9 1.4 dynamic-slice_select_fusion.4
  124.3 1.4 dynamic-slice_select_fusion.2
  125.7 0.0 copy-start
  125.7 0.0 copy-start.1
  125.7 12.4 %fusion.8 = f32[3,16,128]{2,1,0:T(8,128)} fusion(f32[3]{0:T(128)S(1)} %get-tuple-element.29, f32[128,25088]{1,0:T(8,128)} %get-tuple-element.21, f32[128,25088]{1,0:T(8,128)} %get-tuple-element.20, bf16[16,25088]{1,0:T(8,128)(2,1)} %get-tuple-element.11), kind=kOutput, calls=%fused_computation.15 | convolution fusion | flops 337182720 | bytes 26517516 | tf_op jit(solution)/shard_map/egk,sk->esg/dot_general | solution.py:37
  138.1 0.0 copy-done
  138.1 3.5 %copy-done.1 = f32[128,25088]{1,0:T(8,128)S(1)} copy-done((f32[128,25088]{1,0:T(8,128)S(1)}, f32[128,25088]{1,0:T(8,128)}, u32[]{:S(2)}) %copy-start.1) | copy-done | bytes 12845080
  141.6 0.0 copy-start.9
  141.6 6.9 %fusion.7 = f32[3,16,128]{2,1,0:T(8,128)S(1)} fusion(f32[3]{0:T(128)S(1)} %get-tuple-element.28, f32[128,25088]{1,0:T(8,128)S(1)} %copy-done.1, f32[128,25088]{1,0:T(8,128)S(1)} %copy-done, bf16[16,25088]{1,0:T(8,128)(2,1)} %get-tuple-element.12), kind=kOutput, calls=%fused_computation.14 | convolution fusion | flops 337182720 | bytes 26517516 | tf_op jit(solution)/shard_map/egk,sk->esg/dot_general | solution.py:37
  148.5 0.0 copy-done.9
  148.5 0.8 dynamic-slice_select_fusion
  149.3 6.8 %fusion.6 = f32[3,16,128]{2,1,0:T(8,128)S(1)} fusion(f32[3]{0:T(128)S(1)} %get-tuple-element.31, f32[128,25088]{1,0:T(8,128)S(1)} %copy-done.1, f32[128,25088]{1,0:T(8,128)S(1)} %copy-done, bf16[16,25088]{1,0:T(8,128)(2,1)} %get-tuple-element.13), kind=kOutput, calls=%fused_computation.13 | convolution fusion | flops 337182720 | bytes 26517516 | tf_op jit(solution)/shard_map/egk,sk->esg/dot_general | solution.py:37
  156.1 0.0 copy-start.8
  156.1 5.2 %fusion.5 = f32[3,16,128]{2,1,0:T(8,128)S(1)} fusion(f32[3]{0:T(128)S(1)} %get-tuple-element.27, f32[128,25088]{1,0:T(8,128)S(1)} %copy-done.1, f32[128,25088]{1,0:T(8,128)S(1)} %copy-done, bf16[16,25088]{1,0:T(8,128)(2,1)S(1)} %copy-done.9), kind=kOutput, calls=%fused_computation.12 | convolution fusion | flops 337182720 | bytes 26517516 | tf_op jit(solution)/shard_map/egk,sk->esg/dot_general | solution.py:37
  161.3 0.0 copy-done.8
  161.3 0.0 copy-start.3
  161.3 0.0 copy-start.4
  161.3 0.0 copy-start.5
  161.4 0.0 copy-start.2
  161.4 6.8 %fusion.9 = f32[3,16,128]{2,1,0:T(8,128)S(1)} fusion(f32[128,25088]{1,0:T(8,128)S(1)} %copy-done.1, f32[3]{0:T(128)S(1)} %copy-done.8, f32[128,25088]{1,0:T(8,128)S(1)} %copy-done, bf16[16,25088]{1,0:T(8,128)(2,1)} %get-tuple-element.10), kind=kOutput, calls=%fused_computation.16 | convolution fusion | flops 337182720 | bytes 26517516 | tf_op jit(solution)/shard_map/egk,sk->esg/dot_general | solution.py:37
  168.2 0.0 copy-done.3
  168.2 0.0 copy-done.4
  168.2 0.0 copy-done.5
  168.2 16.2 %all-reduce.1 = (bf16[16,128]{1,0:T(8,128)(2,1)S(1)}, bf16[16,128]{1,0:T(8,128)(2,1)S(1)}, bf16[16,128]{1,0:T(8,128)(2,1)S(1)}, bf16[16,128]{1,0:T(8,128)(2,1)S(1)}, bf16[16,128]{1,0:T(8,128)(2,1)S(1)}) all-reduce(bf16[16,128]{1,0:T(8,128)(2,1)S(1)} %copy-done.5, ...), channel_id=1, replica_groups=mesh['ga'=8,'gp'=4] {'gp'}, use_global_device_ids=true, to_apply=%region_2.3 | all-reduce | flops 10240 | bytes 40960 | tf_op jit(solution)/shard_map/psum | solution.py:9
  184.4 0.1 fusion.20
  184.5 0.0 copy-done.2
  184.5 0.1 convolution_add_fusion.3
  184.7 0.1 convolution_add_fusion.2
  184.8 0.1 convolution_add_fusion.1
  185.0 0.1 fusion.10
  185.1 14.3 %psum.94 = f32[3,16,16]{1,2,0:T(8,128)S(1)} all-reduce(f32[3,16,16]{1,2,0:T(8,128)S(1)} %fusion.10), channel_id=1, replica_groups=mesh['ga'=8,'gp'=4] {'gp'}, use_global_device_ids=true, to_apply=%region_15.16 | all-reduce | flops 768 | bytes 6144 | tf_op jit(solution)/shard_map/psum | solution.py:41
  199.4 26.0 %psum.95 = f32[3,16,16]{1,2,0:T(8,128)S(1)} all-reduce(f32[3,16,16]{1,2,0:T(8,128)S(1)} %psum.94), channel_id=1, replica_groups=mesh['ga'=8,'gp'=4] {'ga'}, use_global_device_ids=true, to_apply=%region_16.17 | all-reduce | flops 768 | bytes 6144 | tf_op jit(solution)/shard_map/psum | solution.py:41
  225.3 0.7 copy.8
Async XLA Ops:
  6.5 116.4 %all-reduce.4.cloned.1.call-start = ((), (), s32[]{:S(2)}) async-start(), calls=%async_computation | async-start | bytes 8028160 | tf_op jit(solution)/shard_map/psum | solution.py:9
  26.2 18.8 %copy-start.6 = (f32[16]{0:T(128)S(1)}, f32[16]{0:T(128)}, u32[]{:S(2)}) copy-start(f32[16]{0:T(128)} %param.10) | copy-start | bytes 196
  26.2 19.4 %copy-start.7 = (f32[3]{0:T(128)S(1)}, f32[3]{0:T(128)}, u32[]{:S(2)}) copy-start(f32[3]{0:T(128)} %param.11) | copy-start | bytes 40
  125.7 12.4 %copy-start = (f32[128,25088]{1,0:T(8,128)S(1)}, f32[128,25088]{1,0:T(8,128)}, u32[]{:S(2)}) copy-start(f32[128,25088]{1,0:T(8,128)} %get-tuple-element.20) | copy-start | bytes 38535172
  125.7 15.9 %copy-start.1 = (f32[128,25088]{1,0:T(8,128)S(1)}, f32[128,25088]{1,0:T(8,128)}, u32[]{:S(2)}) copy-start(f32[128,25088]{1,0:T(8,128)} %get-tuple-element.21) | copy-start | bytes 38535172
  141.6 6.9 %copy-start.9 = (bf16[16,25088]{1,0:T(8,128)(2,1)S(1)}, bf16[16,25088]{1,0:T(8,128)(2,1)}, u32[]{:S(2)}) copy-start(bf16[16,25088]{1,0:T(8,128)(2,1)} %get-tuple-element.14) | copy-start | bytes 2408452
  156.1 5.2 %copy-start.8 = (f32[3]{0:T(128)S(1)}, f32[3]{0:T(128)}, u32[]{:S(2)}) copy-start(f32[3]{0:T(128)} %get-tuple-element.30) | copy-start | bytes 40
  161.3 6.9 %copy-start.3 = (bf16[16,128]{1,0:T(8,128)(2,1)S(1)}, bf16[16,128]{1,0:T(8,128)(2,1)}, u32[]{:S(2)}) copy-start(bf16[16,128]{1,0:T(8,128)(2,1)} %get-tuple-element.44) | copy-start | bytes 12292
  161.3 6.9 %copy-start.4 = (bf16[16,128]{1,0:T(8,128)(2,1)S(1)}, bf16[16,128]{1,0:T(8,128)(2,1)}, u32[]{:S(2)}) copy-start(bf16[16,128]{1,0:T(8,128)(2,1)} %get-tuple-element.45) | copy-start | bytes 12292
  161.3 6.9 %copy-start.5 = (bf16[16,128]{1,0:T(8,128)(2,1)S(1)}, bf16[16,128]{1,0:T(8,128)(2,1)}, u32[]{:S(2)}) copy-start(bf16[16,128]{1,0:T(8,128)(2,1)} %dynamic-slice_select_fusion.4) | copy-start | bytes 12292
  161.4 23.2 %copy-start.2 = (f32[3,16,128]{2,1,0:T(8,128)S(1)}, f32[3,16,128]{2,1,0:T(8,128)}, u32[]{:S(2)}) copy-start(f32[3,16,128]{2,1,0:T(8,128)} %fusion.8) | copy-start | bytes 73732
Sparse Core Ops, SparseCore 0:
  26.3 96.5 all-reduce.3
